TPU v7x, 32 devices: a whole 2x2x4 slice. The times are simulated.
32 devices in a mesh: site: 2 (over y), rows: 8 (over z, core), width: 2 (over x).
Axes of the slice: x: 2, y: 2, z: 4, core: 2. Of those that a mesh axis runs over, the one named last changes fastest.
Arguments:
- one_query: float32 [14336, 7168], P(('site', 'rows'), 'width'), parts along dimension 0, may hold values from -0.09375 to 0.09375
- other_query: float32 [14336, 7168], P(('site', 'rows'), 'width'), parts along dimension 0, may hold values from -0.0625 to 0.0625
- one_key: float32 [14336, 1024], P(('site', 'rows'), 'width'), parts along dimension 0, may hold values from -0.09375 to 0.09375
- other_key: float32 [14336, 1024], P(('site', 'rows'), 'width'), parts along dimension 0, may hold values from -0.0625 to 0.0625
- one_value: float32 [14336, 1024], P(('site', 'rows'), 'width'), parts along dimension 0, may hold values from -0.09375 to 0.09375
- other_value: float32 [14336, 1024], P(('site', 'rows'), 'width'), parts along dimension 0, may hold values from -0.0625 to 0.0625
- mix_share: float32 [14336], P(('site', 'rows')), parts along dimension 0, may hold values from 0.2 to 0.8
- norm_train: float32 [14336], P(('site', 'rows', 'width')), parts along dimension 0, may hold values from 0.25 to 1.75
- norm_step: float32 [14336], P(('site', 'rows', 'width')), parts along dimension 0, may hold values from -0.3 to 0.3
Outputs:
- serving_query: bfloat16 [14336, 7168], P('site', 'width'), parts along dimension 0
- serving_key: bfloat16 [14336, 1024], P('site', 'width'), parts along dimension 0
- serving_value: bfloat16 [14336, 1024], P('site', 'width'), parts along dimension 0
- scale_query: float32 [14336], P(('site', 'width')), parts along dimension 0
- scale_key: float32 [2048], P(('site', 'width')), parts along dimension 0
- scale_value: float32 [2048], P(('site', 'width')), parts along dimension 0
- serve_norm: bfloat16 [14336], P('site'), parts along dimension 0
There are 2 independent parts, one for each index of `site`. A program takes and returns all parts, laid end to end along the dimension named above; each array names one. Nothing has to cross between parts.
All inputs are finite; a program needn't handle non-finite values. Where the computation divides by a largest or mean magnitude, that divisor is 1e-20 or more.
Results may differ from a plain program's by a relative error of at most 0.001.
Values may be sent and summed in bfloat16 or wider, within the bound.
A program may use at most 256 MiB of HBM per device.

v0:
```python
import jax
import jax.numpy as jnp
from jax import lax
from jax.sharding import PartitionSpec as P


def shards(
    one_query,
    other_query,
    one_key,
    other_key,
    one_value,
    other_value,
    mix_share,
    norm_train,
    norm_step,
):
    whole_query = mix_share[:, None] * one_query + (1.0 - mix_share[:, None]) * other_query
    whole_key = mix_share[:, None] * one_key + (1.0 - mix_share[:, None]) * other_key
    whole_value = mix_share[:, None] * one_value + (1.0 - mix_share[:, None]) * other_value
    scale_query, scale_key, scale_value = lax.pmax(
        (
            jnp.max(jnp.abs(whole_query), axis=0),
            jnp.max(jnp.abs(whole_key), axis=0),
            jnp.max(jnp.abs(whole_value), axis=0),
        ),
        "rows",
    )
    narrow_query, narrow_key, narrow_value = (
        (whole_query / scale_query).astype(jnp.bfloat16),
        (whole_key / scale_key).astype(jnp.bfloat16),
        (whole_value / scale_value).astype(jnp.bfloat16),
    )
    serving_query, serving_key, serving_value = (
        lax.all_gather(narrow_query, "rows", axis=0, tiled=True),
        lax.all_gather(narrow_key, "rows", axis=0, tiled=True),
        lax.all_gather(narrow_value, "rows", axis=0, tiled=True),
    )
    serve_norm = lax.all_gather(
        (norm_train + norm_step).astype(jnp.bfloat16), ("rows", "width"), axis=0, tiled=True
    )
    return (
        serving_query,
        serving_key,
        serving_value,
        scale_query,
        scale_key,
        scale_value,
        serve_norm,
    )


def solution(mesh):
    in_specs = (
        P(("site", "rows"), "width"),
        P(("site", "rows"), "width"),
        P(("site", "rows"), "width"),
        P(("site", "rows"), "width"),
        P(("site", "rows"), "width"),
        P(("site", "rows"), "width"),
        P(("site", "rows")),
        P(("site", "rows", "width")),
        P(("site", "rows", "width")),
    )
    out_specs = (
        P("site", "width"),
        P("site", "width"),
        P("site", "width"),
        P(("site", "width")),
        P(("site", "width")),
        P(("site", "width")),
        P("site"),
    )
    return jax.shard_map(shards, mesh=mesh, in_specs=in_specs, out_specs=out_specs, check_vma=False)
```

profile of v0, /device:TPU:0, one launch (start us, length us, event | category | flops | bytes accessed | tf_op | source)
XLA Modules:
  0.0 688.0 jit_solution(8904250623209945334)
XLA Ops:
  7.2 0.0 all-gather.6.cloned.1.call-start
  7.2 0.7 broadcast_subtract_fusion
  7.9 0.0 copy-start.1
  7.9 0.0 copy-start.2
  7.9 0.0 copy-start.3
  7.9 0.0 copy-start.4
  7.9 0.0 copy-start.5
  7.9 9.6 %abs_reduce_fusion = f32[3584]{0:T(1024)S(1)} fusion(f32[896,3584]{1,0:T(8,128)} %param.10, f32[896]{0:T(1024)S(1)} %broadcast_subtract_fusion, f32[896,3584]{1,0:T(8,128)} %param.9, f32[896]{0:T(1024)} %param.15), kind=kLoop, calls=%fused_computation.1 | loop fusion | flops 16052736 | bytes 25711616 | tf_op jit(solution)/shard_map/reduce_max | solution.py:23
  17.5 0.0 copy-done.1
  17.5 0.0 copy-done.2
  17.5 0.4 copy-done.3
  17.9 0.5 copy-done.4
  18.5 0.0 copy-done.5
  18.5 0.6 abs_reduce_fusion.1
  19.1 30.3 %all-reduce.1 = (f32[3584]{0:T(1024)S(1)}, f32[512]{0:T(512)S(1)}, f32[512]{0:T(512)S(1)}) all-reduce(f32[3584]{0:T(1024)S(1)} %abs_reduce_fusion, f32[512]{0:T(512)S(1)} %get-tuple-element.8, f32[512]{0:T(512)S(1)} %get-tuple-element.7), channel_id=1, replica_groups=mesh['site'=2,'rows'=8,'width'=2] {'rows'}, use_global_device_ids=true, to_apply=%region_1.0 | all-reduce | flops 4608 | bytes 36864 | tf_op jit(solution)/shard_map/pmax | solution.py:21
  49.4 0.0 copy-start.7
  49.4 0.0 copy-start.8
  49.4 0.0 copy-start.6
  49.4 4.5 divide_convert_fusion.1
  53.8 0.0 copy-done.7
  53.8 0.0 copy-done.8
  53.8 0.0 all-gather.6.cloned.1.call-update
  53.9 0.0 all-gather.8.cloned.1.call-start
  53.9 0.7 all-gather.8.cloned.1.call-update
  54.6 0.0 all-gather.4.cloned.1.call-start
  54.7 0.0 copy-done.6
  54.7 13.6 %divide_convert_fusion = bf16[896,3584]{1,0:T(8,128)(2,1)} fusion(f32[3584]{0:T(1024)S(1)} %get-tuple-element.24, f32[896,3584]{1,0:T(8,128)} %param.10, f32[896]{0:T(1024)S(1)} %broadcast_subtract_fusion, f32[896,3584]{1,0:T(8,128)} %param.9, f32[896]{0:T(1024)S(1)} %copy-done.5), kind=kLoop, calls=%fused_computation | loop fusion | flops 16056320 | bytes 32134144 | tf_op jit(solution)/shard_map/convert_element_type | solution.py:30
  68.2 0.0 copy-start.11
  68.2 0.0 copy-start.9
  68.2 0.0 copy-start.10
  68.3 0.0 all-gather.4.cloned.1.call-update
  68.3 0.6 copy-done.11
  68.9 0.6 dynamic-slice
  70.1 0.0 copy-done.9
  70.1 0.0 copy-done.10
  70.2 0.3 dynamic-update-slice
  70.4 62.5 %all-reduce = bf16[7168]{0:T(1024)(128)(2,1)} all-reduce(bf16[7168]{0:T(1024)(128)(2,1)S(1)} %dynamic-update-slice), channel_id=1, replica_groups=mesh['site'=2,'rows'=8,'width'=2] {'rows','width'}, use_global_device_ids=true, to_apply=%add | all-reduce | flops 7168 | bytes 28672
  133.0 0.0 all-gather.6.cloned.1.call-done
  133.0 67.2 %all-gather.8.cloned.1.call-done = bf16[7168,512]{1,0:T(8,128)(2,1)} async-done(((bf16[896,512]{1,0:T(8,128)(2,1)}), bf16[7168,512]{1,0:T(8,128)(2,1)}) %all-gather.8.cloned.1.call-update) | async-done | bytes 7340048 | tf_op jit(solution)/shard_map/all_gather | solution.py:37
  200.2 436.7 %all-gather.4.cloned.1.call-done = bf16[7168,3584]{1,0:T(8,128)(2,1)} async-done(((bf16[896,3584]{1,0:T(8,128)(2,1)}), bf16[7168,3584]{1,0:T(8,128)(2,1)}) %all-gather.4.cloned.1.call-update) | async-done | bytes 51380240 | tf_op jit(solution)/shard_map/all_gather | solution.py:35
  636.9 34.8 %copy.20 = bf16[7168,3584]{1,0:T(8,128)(2,1)} copy(bf16[7168,3584]{1,0:T(8,128)(2,1)} %all-gather.4.cloned.1.call-done) | data formatting | bytes 102760448
  671.7 0.0 copy-start
  671.7 6.8 copy.21
  678.5 0.0 copy-done
  678.5 3.0 copy.22
  (2 shorter events, 0.0 us)
Async XLA Ops:
  7.2 125.8 %all-gather.6.cloned.1.call-start = ((), (), s32[]{:S(2)}) async-start(), calls=%async_computation.1 | async-start | bytes 8257536 | tf_op jit(solution)/shard_map/all_gather | solution.py:36
  7.9 9.6 %copy-start.1 = (f32[896,512]{1,0:T(8,128)S(1)}, f32[896,512]{1,0:T(8,128)}, u32[]{:S(2)}) copy-start(f32[896,512]{1,0:T(8,128)} %param.14) | copy-start | bytes 5505028
  7.9 9.6 %copy-start.2 = (f32[896,512]{1,0:T(8,128)S(1)}, f32[896,512]{1,0:T(8,128)}, u32[]{:S(2)}) copy-start(f32[896,512]{1,0:T(8,128)} %param.13) | copy-start | bytes 5505028
  7.9 10.0 %copy-start.3 = (f32[896,512]{1,0:T(8,128)S(1)}, f32[896,512]{1,0:T(8,128)}, u32[]{:S(2)}) copy-start(f32[896,512]{1,0:T(8,128)} %param.12) | copy-start | bytes 5505028
  7.9 10.5 %copy-start.4 = (f32[896,512]{1,0:T(8,128)S(1)}, f32[896,512]{1,0:T(8,128)}, u32[]{:S(2)}) copy-start(f32[896,512]{1,0:T(8,128)} %param.11) | copy-start | bytes 5505028
  7.9 10.5 %copy-start.5 = (f32[896]{0:T(1024)S(1)}, f32[896]{0:T(1024)}, u32[]{:S(2)}) copy-start(f32[896]{0:T(1024)} %param.15) | copy-start | bytes 10756
  49.4 4.5 copy-start.7
  49.4 4.5 copy-start.8
  49.4 5.3 copy-start.6
  53.9 146.3 %all-gather.8.cloned.1.call-start = ((), (), s32[]{:S(2)}) async-start(), calls=%async_computation.2 | async-start | bytes 8257536 | tf_op jit(solution)/shard_map/all_gather | solution.py:37
  54.6 582.3 %all-gather.4.cloned.1.call-start = ((), (), s32[]{:S(2)}) async-start(), calls=%async_computation | async-start | bytes 57802752 | tf_op jit(solution)/shard_map/all_gather | solution.py:35
  68.2 0.7 copy-start.11
  68.2 1.9 copy-start.9
  68.2 1.9 copy-start.10
  671.7 6.8 copy-start
Sparse Core Ops, SparseCore 0:
  54.0 72.0 all-gather.5
  128.3 71.8 all-gather.7
  202.4 434.4 all-gather.3
where the time goes:
time: 688 us
  waiting for transfers between devices  505 us (73%)
  blocking collectives  92.8 us (13%)
  local copies, waits for them, and re-layouts  47 us (7%)
  other arithmetic  28.9 us (4%)
  between operations  14.5 us (2%)
    all_gather x1, waiting for transfers between devices, shards(): lax.all_gather(narrow_query, 'rows', axis=0, tiled=True)  437 us
    all_gather x1, waiting for transfers between devices, shards(): lax.all_gather(narrow_value, 'rows', axis=0, tiled=True)  67.2 us
    unnamed x1, blocking collectives  62.5 us
    unnamed x30, local copies, waits for them, and re-layouts  47 us
    pmax x1, blocking collectives, shards(): lax.pmax((jnp.max(jnp.abs(whole_query), axis=0), jnp.max(jnp.abs(whole_ke...  30.3 us
  transfers between devices with their start and end apart: 3, of which 2 were waited for; matrix products, arithmetic and copies ran while one was open for 2% of the time, Pallas kernels for 0%

commit v1 on v0

v1 whole, which is shorter than its diff:
```python
import functools

import jax
import jax.numpy as jnp
from jax import lax
from jax.experimental import pallas as pl
from jax.experimental.pallas import tpu as pltpu
from jax.sharding import PartitionSpec as P

MESH = pl.DeviceIdType.MESH
CORES = 2


def merge(
    ranks,
    widths,
    one_query,
    other_query,
    one_key,
    other_key,
    one_value,
    other_value,
    mix,
    norm_train,
    norm_step,
    query,
    key,
    value,
    scale_query,
    scale_key,
    scale_value,
    norms,
    one,
    other,
    narrow,
    peaks,
    load_sem,
    out_sem,
    peak_send,
    peak_recv,
    norm_send,
    norm_recv,
    up_send,
    up_recv,
    down_send,
    down_recv,
    side_send,
    side_recv,
):
    depth, span = one_key.shape
    parts = one_query.shape[1] // span
    chips = ranks // CORES
    me = lax.axis_index("rows")
    across = lax.axis_index("width")
    chip, core = me // CORES, me % CORES
    partner = chip * CORES + 1 - core
    group = ranks * widths
    block = 32 if depth % 32 == 0 else depth

    def loads(k):
        if isinstance(k, int) and k >= parts:
            sources = (one_key, other_key) if k == parts else (one_value, other_value)
        else:
            cut = pl.ds(pl.multiple_of(k * span, span), span)
            sources = one_query.at[:, cut], other_query.at[:, cut]
        return [
            pltpu.make_async_copy(source, target.at[k], load_sem.at[i, k])
            for i, (source, target) in enumerate(zip(sources, (one, other)))
        ]

    def each_part(body):
        pl.loop(0, parts)(body)

    @each_part
    def _(k):
        for copy in loads(k):
            copy.start()

    for k in (parts, parts + 1):
        for copy in loads(k):
            copy.start()

    barrier = pltpu.get_barrier_semaphore()
    mine = me * widths + across

    @pl.loop(1, group)
    def _(step):
        to = lax.rem(mine + step, group)
        pl.semaphore_signal(
            barrier,
            inc=1,
            device_id={"rows": to // widths, "width": lax.rem(to, widths)},
            device_id_type=MESH,
        )

    norms[mine] = norm_train[...] + norm_step[...]
    pl.semaphore_wait(barrier, group - 1)

    @pl.loop(1, group)
    def _(step):
        to = lax.rem(mine + step, group)
        pltpu.make_async_remote_copy(
            src_ref=norms.at[mine],
            dst_ref=norms.at[mine],
            send_sem=norm_send,
            recv_sem=norm_recv,
            device_id={"rows": to // widths, "width": lax.rem(to, widths)},
            device_id_type=MESH,
        ).start()

    def mixed(k):
        for copy in loads(k):
            copy.wait()

        def step(b, top):
            rows = pl.ds(pl.multiple_of(b * block, block), block)
            share = mix[rows]
            whole = share * one[k, rows] + (1.0 - share) * other[k, rows]
            one[k, rows] = whole
            return jnp.maximum(top, jnp.max(jnp.abs(whole).reshape(-1, 8, span), axis=0))

        top = lax.fori_loop(0, depth // block, step, jnp.zeros((8, span), jnp.float32))
        peaks[k, me] = jnp.max(top, axis=0, keepdims=True)

        @pl.loop(1, ranks)
        def _(step):
            pltpu.make_async_remote_copy(
                src_ref=peaks.at[k, me],
                dst_ref=peaks.at[k, me],
                send_sem=peak_send.at[k],
                recv_sem=peak_recv.at[k],
                device_id={"rows": lax.rem(me + step, ranks)},
                device_id_type=MESH,
            ).start()

    def slot(k, rank):
        rows = pl.ds(pl.multiple_of(rank * depth, depth), depth)
        if isinstance(k, int) and k == parts:
            return key.at[rows]
        return query.at[rows, pl.ds(pl.multiple_of(k * span, span), span)]

    def send(k, rank, to, send_sem, recv_sem):
        return pltpu.make_async_remote_copy(
            src_ref=slot(k, rank),
            dst_ref=slot(k, rank),
            send_sem=send_sem,
            recv_sem=recv_sem,
            device_id={"rows": to},
            device_id_type=MESH,
        )

    def go_up(k, hop):
        return send(k, me - CORES * hop, me + CORES, up_send.at[hop, k], up_recv.at[hop, k])

    def go_down(k, hop):
        return send(k, me + CORES * hop, me - CORES, down_send.at[hop, k], down_recv.at[hop, k])

    def go_side(k, hop):
        index = hop + chips - 1
        return send(k, me + CORES * hop, partner, side_send.at[index, k], side_recv.at[index, k])

    def from_side(k, hop):
        index = hop + chips - 1
        return send(
            k, partner + CORES * hop, partner, side_send.at[index, k], side_recv.at[index, k]
        )

    def from_below(k, hop):
        return send(k, me - CORES * (hop + 1), me - CORES, up_send.at[hop, k], up_recv.at[hop, k])

    def from_above(k, hop):
        return send(
            k, me + CORES * (hop + 1), me + CORES, down_send.at[hop, k], down_recv.at[hop, k]
        )

    has_below, has_above = chip >= 1, chip < chips - 1

    def scaled(k, scale_ref, cut):
        everyone = peaks.at[k, pl.ds(0, ranks - 1)]
        pltpu.make_async_copy(everyone, everyone, peak_recv.at[k]).wait()
        scale = jnp.max(peaks[k], axis=0)
        scale_ref[:, cut] = scale

        @pl.loop(0, depth // block)
        def _(b):
            rows = pl.ds(pl.multiple_of(b * block, block), block)
            narrow[k, rows] = (one[k, rows] / scale).astype(jnp.bfloat16)

        target = value if isinstance(k, int) and k > parts else slot(k, me)
        copy = pltpu.make_async_copy(narrow.at[k], target, out_sem.at[k])
        copy.start()
        if isinstance(k, int) and k > parts:
            copy.wait()
            return
        copy.wait()

        @pl.when(has_above)
        def _():
            go_up(k, 0).start()

        @pl.when(has_below)
        def _():
            go_down(k, 0).start()

        go_side(k, 0).start()

    lag = min(2, parts)
    pl.loop(0, lag)(mixed)

    def part_cut(k):
        return pl.ds(pl.multiple_of(k * span, span), span)

    @pl.loop(0, parts - lag)
    def _(k):
        mixed(k + lag)
        scaled(k, scale_query, part_cut(k))

    mixed(parts)
    mixed(parts + 1)

    @pl.loop(parts - lag, parts)
    def _(k):
        scaled(k, scale_query, part_cut(k))

    scaled(parts, scale_key, slice(None))
    scaled(parts + 1, scale_value, slice(None))

    def relay(k, hop):
        @pl.when(chip >= hop)
        def _():
            from_below(k, hop - 1).wait_recv()

            @pl.when(has_above)
            def _():
                go_up(k, hop).start()

            go_side(k, -hop).start()

        @pl.when(chip + hop < chips)
        def _():
            from_above(k, hop - 1).wait_recv()

            @pl.when(has_below)
            def _():
                go_down(k, hop).start()

            go_side(k, hop).start()

    @pl.loop(1, chips)
    def _(hop):
        each_part(lambda k: relay(k, hop))
        relay(parts, hop)

    def finish(k):
        @pl.loop(0, chips - 1)
        def _(hop):
            @pl.when((chip >= hop) & has_above)
            def _():
                go_up(k, hop).wait_send()

            @pl.when((chip + hop < chips) & has_below)
            def _():
                go_down(k, hop).wait_send()

        @pl.loop(0, chips)
        def _(origin):
            go_side(k, origin - chip).wait_send()
            from_side(k, origin - chip).wait_recv()

    each_part(finish)
    finish(parts)

    def settle(k):
        everyone = peaks.at[k, pl.ds(0, ranks - 1)]
        pltpu.make_async_copy(everyone, everyone, peak_send.at[k]).wait()

    pl.loop(0, parts + 2)(settle)
    others = norms.at[pl.ds(0, group - 1)]
    pltpu.make_async_copy(others, others, norm_recv).wait()
    pltpu.make_async_copy(others, others, norm_send).wait()


def shards(
    ranks,
    widths,
    one_query,
    other_query,
    one_key,
    other_key,
    one_value,
    other_value,
    mix_share,
    norm_train,
    norm_step,
):
    depth, span = one_key.shape
    wide = one_query.shape[1]
    parts = wide // span
    chips = ranks // CORES
    group = ranks * widths
    bit = norm_train.shape[0]
    shape = jax.ShapeDtypeStruct
    anywhere = pl.BlockSpec(memory_space=pl.ANY)
    near = pl.BlockSpec(memory_space=pltpu.VMEM)
    dma = pltpu.SemaphoreType.DMA
    query, key, value, scale_query, scale_key, scale_value, norms = pl.pallas_call(
        functools.partial(merge, ranks, widths),
        out_shape=(
            shape((ranks * depth, wide), jnp.bfloat16),
            shape((ranks * depth, span), jnp.bfloat16),
            shape((depth, span), jnp.bfloat16),
            shape((1, wide), jnp.float32),
            shape((1, span), jnp.float32),
            shape((1, span), jnp.float32),
            shape((group, 1, bit), jnp.float32),
        ),
        in_specs=[anywhere] * 6 + [near] * 3,
        out_specs=[anywhere] * 3 + [near] * 4,
        scratch_shapes=[
            pltpu.VMEM((parts + 2, depth, span), jnp.float32),
            pltpu.VMEM((parts + 2, depth, span), jnp.float32),
            pltpu.VMEM((parts + 2, depth, span), jnp.bfloat16),
            pltpu.VMEM((parts + 2, ranks, 1, span), jnp.float32),
            dma((2, parts + 2)),
            dma((parts + 2,)),
            dma((parts + 2,)),
            dma((parts + 2,)),
            dma,
            dma,
            dma((chips - 1, parts + 1)),
            dma((chips - 1, parts + 1)),
            dma((chips - 1, parts + 1)),
            dma((chips - 1, parts + 1)),
            dma((2 * chips - 1, parts + 1)),
            dma((2 * chips - 1, parts + 1)),
        ],
        compiler_params=pltpu.CompilerParams(
            collective_id=0, has_side_effects=True, vmem_limit_bytes=56 * 2**20
        ),
    )(
        one_query,
        other_query,
        one_key,
        other_key,
        one_value,
        other_value,
        mix_share[:, None],
        norm_train[None],
        norm_step[None],
    )
    value = lax.all_gather(value, "rows", axis=0, tiled=True)
    return (
        query,
        key,
        value,
        scale_query[0],
        scale_key[0],
        scale_value[0],
        norms.reshape(-1).astype(jnp.bfloat16),
    )


def solution(mesh):
    in_specs = (
        P(("site", "rows"), "width"),
        P(("site", "rows"), "width"),
        P(("site", "rows"), "width"),
        P(("site", "rows"), "width"),
        P(("site", "rows"), "width"),
        P(("site", "rows"), "width"),
        P(("site", "rows")),
        P(("site", "rows", "width")),
        P(("site", "rows", "width")),
    )
    out_specs = (
        P("site", "width"),
        P("site", "width"),
        P("site", "width"),
        P(("site", "width")),
        P(("site", "width")),
        P(("site", "width")),
        P("site"),
    )
    body = functools.partial(shards, mesh.shape["rows"], mesh.shape["width"])
    return jax.shard_map(body, mesh=mesh, in_specs=in_specs, out_specs=out_specs, check_vma=False)
```

time: 688 us -> 630 us (0.916)
  Pallas kernels: 0 us -> 497 us
  waiting for transfers between devices: 505 us -> 69 us
  blocking collectives: 92.8 us -> 0 us
  other arithmetic: 28.9 us -> 2.21 us
    pallas_call x0 -> x1, Pallas kernels: none -> 497 us  [shards(): pl.pallas_call(functools.partial(merge, ranks, widths), out_shape=(shape(...]
    all_gather x3 -> x1, waiting for transfers between devices: 504 us -> 69 us  [shards(): value = lax.all_gather(value, 'rows', axis=0, tiled=True)]
    unnamed x1 -> x0, blocking collectives: 62.5 us -> none
    pmax x1 -> x0, blocking collectives: 30.3 us -> none  [shards(): lax.pmax((jnp.max(jnp.abs(whole_query), axis=0), jnp.max(jnp.abs(whole_ke...]
    convert_element_type x3 -> x1, other arithmetic: 18 us -> 0.85 us  [shards(): norms.reshape(-1).astype(jnp.bfloat16)]
    reduce_max x2 -> x0, other arithmetic: 10.2 us -> none  [the longest x1 9.58 us: shards(): jnp.max(jnp.abs(whole_query), axis=0)]
    unnamed x30 -> x11, local copies, waits for them, and re-layouts: 47 us -> 45.8 us
  transfers between devices with their start and end apart: 3 -> 1, of which waited for: 2 -> 1; matrix products, arithmetic and copies ran while one was open for 2% -> 0% of each run, Pallas kernels for 0% -> 0%
where the time goes in v1:
time: 630 us
  Pallas kernels  497 us (79%)
  waiting for transfers between devices  69 us (11%)
  local copies, waits for them, and re-layouts  48.1 us (8%)
  between operations  14 us (2%)
    pallas_call x1, Pallas kernels, shards(): pl.pallas_call(functools.partial(merge, ranks, widths), out_shape=(shape(...  497 us
    all_gather x1, waiting for transfers between devices, shards(): value = lax.all_gather(value, 'rows', axis=0, tiled=True)  69 us
    unnamed x11, local copies, waits for them, and re-layouts  45.8 us
  transfers between devices with their start and end apart: 1, of which 1 were waited for; matrix products, arithmetic and copies ran while one was open for 0% of the time, Pallas kernels for 0%

profile of v1, /device:TPU:0, one launch (start us, length us, event | category | flops | bytes accessed | tf_op | source)
XLA Modules:
  0.0 629.9 jit_solution(1323708916356510512)
XLA Ops:
  7.2 0.0 all-gather.2.cloned.1.call-start
  7.2 1.6 broadcast_in_dim.12.mix
  8.9 496.5 %shard_map.144 = (bf16[7168,3584]{1,0:T(8,128)(2,1)}, bf16[7168,512]{1,0:T(8,128)(2,1)}, bf16[896,512]{1,0:T(8,128)(2,1)}, f32[1,3584]{1,0:T(1,128)}, f32[1,512]...) custom-call(f32[896,3584]{1,0:T(8,128)} %one_query.1, f32[896,3584]{1,0:T(8,128)} %other_query.1, ...), custom_call_target="tpu_custom_call" | custom-call | tf_op jit(solution)/shard_map/pallas_call | solution.py:306
  505.4 0.0 all-gather.2.cloned.1.call-update
  505.4 0.8 convert_reduce_fusion
  506.3 0.7 convert_element_type.7
  507.0 1.4 reduce
  508.3 69.0 %all-gather.2.cloned.1.call-done = bf16[7168,512]{1,0:T(8,128)(2,1)} async-done(((bf16[896,512]{1,0:T(8,128)(2,1)}), bf16[7168,512]{1,0:T(8,128)(2,1)}) %all-gather.2.cloned.1.call-update) | async-done | bytes 7340048 | tf_op jit(solution)/shard_map/all_gather | solution.py:351
  577.3 34.8 %copy.22 = bf16[7168,3584]{1,0:T(8,128)(2,1)} copy(bf16[7168,3584]{1,0:T(8,128)(2,1)} %get-tuple-element.28) | data formatting | bytes 102760448
  612.1 0.0 copy-start
  612.1 6.8 %copy.23 = bf16[7168,512]{1,0:T(8,128)(2,1)} copy(bf16[7168,512]{1,0:T(8,128)(2,1)} %get-tuple-element.29) | data formatting | bytes 14680064
  618.9 0.0 copy-done
  618.9 0.0 copy-start.2
  618.9 0.0 copy-start.1
  618.9 3.0 copy.24
  621.9 0.0 copy-done.2
  621.9 0.6 copy.25
  622.5 0.0 copy-done.1
  622.5 0.6 copy.26
Async XLA Ops:
  7.2 570.1 %all-gather.2.cloned.1.call-start = ((), (), s32[]{:S(2)}) async-start(), calls=%async_computation | async-start | bytes 8257536 | tf_op jit(solution)/shard_map/all_gather | solution.py:351
  612.1 6.8 %copy-start = (bf16[7168,512]{1,0:T(8,128)(2,1)S(1)}, bf16[7168,512]{1,0:T(8,128)(2,1)}, u32[]{:S(2)}) copy-start(bf16[7168,512]{1,0:T(8,128)(2,1)} %all-gather.2.cloned.1.call-done) | copy-start | bytes 22020100
  618.9 3.1 copy-start.2
  618.9 3.6 copy-start.1
Sparse Core Ops, SparseCore 0:
  505.5 71.7 all-gather.1
